TPU v7x, 32 devices: a whole 2x2x4 slice. The times are simulated.
32 devices in a mesh: section: 2 (over x), expert: 4 (over y, core), dp: 4 (over z).
Axes of the slice: x: 2, y: 2, z: 4, core: 2. Of those that a mesh axis runs over, the one named last changes fastest.
Arguments:
- x_in: bfloat16 [8, 256, 2048], P(None, ('expert', 'dp'), 'section'), may hold values from -6 to 6
- cotangent: bfloat16 [8, 256, 2048], P(None, ('expert', 'dp'), 'section'), may hold values from -6 to 6
- route_ids: int32 [2, 8, 256, 2], P('section', None, ('expert', 'dp')), may hold values from 0 to 15, all different within a row; in each aligned block of 16 rows (0 to 15, 16 to 31, ..., all dimensions but the last counted through in order) at most 2 rows name the same one
- norm_gain: float32 [2, 2048], P('section'), may hold values from 0.5 to 1.5
- router: bfloat16 [2, 2048, 16], P('section'), may hold values from -0.125 to 0.125
- w_gate_up: bfloat16 [2, 16, 2048, 1024], P('section', ('expert', 'dp')), may hold values from -0.125 to 0.125
- w_down: bfloat16 [2, 16, 512, 2048], P('section', ('expert', 'dp')), may hold values from -0.25 to 0.25
Outputs:
- grad_in: bfloat16 [8, 256, 2048], P(None, ('expert', 'dp'), 'section')
- grad_gate_up: float32 [2, 16, 2048, 1024], P('section', ('expert', 'dp'))
- grad_down: float32 [2, 16, 512, 2048], P('section', ('expert', 'dp'))
- grad_router: float32 [2, 2048, 16], P('section')
- grad_gain: float32 [2, 2048], P('section')
Inputs may be any that keep to these rules, and one draw needn't show every extreme that they name: `route_ids`: each row names two different experts; the 16 rows of one device in one layer and micro-batch name any expert at most 2 times, a bound that some block reaches in some of them.
All inputs are finite; a program needn't handle non-finite values.
Results may differ from a plain program's by a relative error of at most 0.035.
Values may be sent and summed in bfloat16 or wider, within the bound.
A program may use at most 64 MiB of HBM per device.

v0:
```python
import jax
import jax.numpy as jnp
from jax import lax
from jax.sharding import PartitionSpec as P

EPS = 1e-05


def shifted(value, axis, steps):
    count = lax.axis_size(axis)
    leading, last = (max(0, -steps), min(count, count - steps))
    return lax.ppermute(value, axis, [(source, source + steps) for source in range(leading, last)])


def keep_row(stash, position, value, active):
    old_row = lax.dynamic_index_in_dim(stash, position, 0, keepdims=False)
    return lax.dynamic_update_index_in_dim(stash, jnp.where(active, value, old_row), position, 0)


def slot_tables(route_rows, n_expert, capacity):
    experts = jnp.arange(n_expert, dtype=jnp.int32)
    expert_hits = (route_rows[:, :, None] == experts).astype(jnp.int32)
    per_expert = jnp.sum(expert_hits, axis=1)
    before = jnp.cumsum(per_expert, axis=0) - per_expert
    slot_ids = jnp.sum(expert_hits * before[:, None, :], axis=2)
    dest_cell = jnp.transpose(route_rows * capacity + slot_ids)
    cell_ids = jnp.arange(n_expert * capacity, dtype=jnp.int32)
    slot_place = (dest_cell[:, :, None] == cell_ids).astype(jnp.bfloat16)
    return (expert_hits.astype(jnp.float32), slot_place)


def norm_rows(layer_in, gain_vec):
    h_wide = layer_in.astype(jnp.float32)
    inv_rms = lax.rsqrt(jnp.mean(h_wide * h_wide, axis=-1, keepdims=True) + EPS)
    normed = (h_wide * inv_rms * gain_vec).astype(jnp.bfloat16)
    return (h_wide, inv_rms, normed)


def pair_gates(normed, router_mat, expert_hits):
    logits = jnp.dot(normed, router_mat, preferred_element_type=jnp.float32)
    chosen = jnp.sum(expert_hits * logits[:, None, :], axis=2)
    return (
        jax.nn.sigmoid(chosen[:, 0] - chosen[:, 1]),
        jax.nn.sigmoid(chosen[:, 1] - chosen[:, 0]),
    )


def expert_inner(exp_rows, w_gu):
    gate_up = jnp.einsum("sekd,edf->sekf", exp_rows, w_gu, preferred_element_type=jnp.float32)
    half_cols = w_gu.shape[2] // 2
    gate_part = gate_up[..., :half_cols]
    up_part = gate_up[..., half_cols:]
    sigmoid_gate = jax.nn.sigmoid(gate_part)
    hidden = (gate_part * sigmoid_gate * up_part).astype(jnp.bfloat16)
    return (gate_part, up_part, sigmoid_gate, hidden)


def expert_grads(gate_part, up_part, sigmoid_gate, dy_rows, w_gu, w_dn):
    d_hidden = jnp.einsum("sekd,efd->sekf", dy_rows, w_dn, preferred_element_type=jnp.float32)
    silu_gate = gate_part * sigmoid_gate
    silu_slope = sigmoid_gate * (1.0 + gate_part * (1.0 - sigmoid_gate))
    gate_up_grad = jnp.concatenate(
        [d_hidden * up_part * silu_slope, d_hidden * silu_gate], axis=-1
    ).astype(jnp.bfloat16)
    rows_grad = jnp.einsum(
        "sekf,edf->sekd", gate_up_grad, w_gu, preferred_element_type=jnp.float32
    ).astype(jnp.bfloat16)
    return (gate_up_grad, rows_grad)


def local(x_in, cotangent, route_ids, norm_gain, router, w_gate_up, w_down):
    micro_count, tok_rows, _ = x_in.shape
    n_segment = lax.axis_size("section")
    n_rank = lax.axis_size("expert") * lax.axis_size("dp")
    per_rank = w_down.shape[1]
    hidden_width = w_down.shape[2]
    model_width = w_down.shape[3]
    n_expert = per_rank * n_rank
    capacity = tok_rows * 2 * 9 // (8 * n_expert)
    cells = n_expert * capacity
    segment_idx = lax.axis_index("section")
    rows_shape = (n_rank, per_rank, capacity, model_width)
    x_all, top_all = (
        lax.all_gather(x_in, "section", axis=2, tiled=True),
        lax.all_gather(cotangent, "section", axis=2, tiled=True),
    )
    route_all = route_ids[0]
    gain_vec = norm_gain[0]
    router_mat = router[0]
    router_wide = router_mat.astype(jnp.float32)
    w_gu = w_gate_up[0]
    w_dn = w_down[0]
    ticks = micro_count + n_segment - 1

    def expert_forward(piece_rows):
        _, _, _, hidden = expert_inner(piece_rows, w_gu)
        out_rows = jnp.einsum(
            "sekf,efd->sekd", hidden, w_dn, preferred_element_type=jnp.float32
        ).astype(jnp.bfloat16)
        return (
            lax.all_to_all(out_rows, ("expert", "dp"), split_axis=0, concat_axis=0, tiled=True),
            piece_rows,
        )

    def forward_tick(tick_no, state_in):
        received, stash_h, stash_y, stash_x = state_in
        tick_slot = tick_no - segment_idx
        active = (tick_slot >= 0) & (tick_slot < micro_count)
        micro_idx = jnp.clip(tick_slot, 0, micro_count - 1)
        fresh_in = lax.dynamic_index_in_dim(x_all, micro_idx, 0, keepdims=False)
        layer_in = jnp.where(segment_idx == 0, fresh_in, received)
        h_wide, inv_rms, normed = norm_rows(layer_in, gain_vec)
        route_rows = lax.dynamic_index_in_dim(route_all, micro_idx, 0, keepdims=False)
        expert_hits, slot_place = slot_tables(route_rows, n_expert, capacity)
        send_rows = jnp.einsum("ktc,td->cd", slot_place, normed, preferred_element_type=jnp.float32)
        send_rows = send_rows.astype(jnp.bfloat16).reshape(rows_shape)
        returned, landed = expert_forward(
            lax.all_to_all(send_rows, ("expert", "dp"), split_axis=0, concat_axis=0, tiled=True)
        )
        back_flat = returned.reshape(cells, model_width)
        picked = jnp.einsum(
            "ktc,cd->ktd", slot_place, back_flat, preferred_element_type=jnp.float32
        )
        first_gate, second_gate = pair_gates(normed, router_mat, expert_hits)
        layer_out = (
            h_wide + first_gate[:, None] * picked[0] + second_gate[:, None] * picked[1]
        ).astype(jnp.bfloat16)
        passed = shifted(layer_out, "section", 1)
        stash_h = keep_row(stash_h, micro_idx, layer_in, active)
        stash_y = keep_row(stash_y, micro_idx, back_flat, active)
        stash_x = keep_row(stash_x, micro_idx, landed, active)
        return (passed, stash_h, stash_y, stash_x)

    start_fwd = (
        jnp.zeros((tok_rows, model_width), jnp.bfloat16),
        jnp.zeros((micro_count, tok_rows, model_width), jnp.bfloat16),
        jnp.zeros((micro_count, cells, model_width), jnp.bfloat16),
        jnp.zeros((micro_count,) + rows_shape, jnp.bfloat16),
    )
    _, stash_h, stash_y, stash_x = lax.fori_loop(0, ticks, forward_tick, start_fwd)

    def backward_tick(tick_no, state_in):
        received, keep_rows, keep_dy, keep_hidden, keep_dab, stash_grad, acc_router, acc_gain = (
            state_in
        )
        tick_slot = tick_no - (n_segment - 1 - segment_idx)
        active = (tick_slot >= 0) & (tick_slot < micro_count)
        micro_idx = jnp.clip(tick_slot, 0, micro_count - 1)
        fresh_top = lax.dynamic_index_in_dim(top_all, micro_idx, 0, keepdims=False)
        grad_top = jnp.where(segment_idx == n_segment - 1, fresh_top, received)
        grad_wide = grad_top.astype(jnp.float32)
        layer_in = lax.dynamic_index_in_dim(stash_h, micro_idx, 0, keepdims=False)
        h_wide, inv_rms, normed = norm_rows(layer_in, gain_vec)
        route_rows = lax.dynamic_index_in_dim(route_all, micro_idx, 0, keepdims=False)
        expert_hits, slot_place = slot_tables(route_rows, n_expert, capacity)
        first_gate, second_gate = pair_gates(normed, router_mat, expert_hits)
        gates = jnp.stack([first_gate, second_gate])
        scaled = (gates[:, :, None] * grad_wide[None]).astype(jnp.bfloat16)
        dy_send = jnp.einsum("ktc,ktd->cd", slot_place, scaled, preferred_element_type=jnp.float32)
        dy_send = dy_send.astype(jnp.bfloat16).reshape(rows_shape)
        exp_rows = lax.dynamic_index_in_dim(stash_x, micro_idx, 0, keepdims=False)
        dy_rows = lax.all_to_all(dy_send, ("expert", "dp"), split_axis=0, concat_axis=0, tiled=True)
        gate_part, up_part, sigmoid_gate, hidden = expert_inner(exp_rows, w_gu)
        gate_up_grad, rows_grad = expert_grads(
            gate_part, up_part, sigmoid_gate, dy_rows, w_gu, w_dn
        )
        back_grad = lax.all_to_all(
            rows_grad, ("expert", "dp"), split_axis=0, concat_axis=0, tiled=True
        )
        back_y = lax.dynamic_index_in_dim(stash_y, micro_idx, 0, keepdims=False)
        keep_dy = keep_row(keep_dy, micro_idx, dy_rows, active)
        keep_hidden = keep_row(keep_hidden, micro_idx, hidden, active)
        keep_dab = keep_row(keep_dab, micro_idx, gate_up_grad, active)
        normed_grad = jnp.einsum(
            "ktc,cd->td",
            slot_place,
            back_grad.reshape(cells, model_width),
            preferred_element_type=jnp.float32,
        )
        picked = jnp.einsum("ktc,cd->ktd", slot_place, back_y, preferred_element_type=jnp.float32)
        gate_grad = jnp.sum(grad_wide[None] * picked, axis=-1)
        logit_grad = first_gate * second_gate * (gate_grad[0] - gate_grad[1])
        logit_cols = logit_grad[:, None] * (expert_hits[:, 0, :] - expert_hits[:, 1, :])
        normed_grad = normed_grad + jnp.dot(
            logit_cols, router_wide.T, precision=lax.Precision.HIGHEST
        )
        router_term = jnp.dot(
            normed.astype(jnp.float32).T, logit_cols, precision=lax.Precision.HIGHEST
        )
        acc_router = acc_router + jnp.where(active, router_term, 0.0)
        acc_gain = acc_gain + jnp.where(
            active, jnp.sum(normed_grad * h_wide * inv_rms, axis=0), 0.0
        )
        scaled_grad = normed_grad * gain_vec
        projection = jnp.mean(scaled_grad * h_wide, axis=-1, keepdims=True)
        input_grad = (
            grad_wide + inv_rms * scaled_grad - h_wide * inv_rms * inv_rms * inv_rms * projection
        )
        grad_sent = input_grad.astype(jnp.bfloat16)
        stash_grad = keep_row(stash_grad, micro_idx, grad_sent, active)
        passed = shifted(grad_sent, "section", -1)
        return (passed, keep_rows, keep_dy, keep_hidden, keep_dab, stash_grad, acc_router, acc_gain)

    start_bwd = (
        jnp.zeros((tok_rows, model_width), jnp.bfloat16),
        stash_x,
        jnp.zeros((micro_count,) + rows_shape, jnp.bfloat16),
        jnp.zeros((micro_count, n_rank, per_rank, capacity, hidden_width), jnp.bfloat16),
        jnp.zeros((micro_count, n_rank, per_rank, capacity, 2 * hidden_width), jnp.bfloat16),
        jnp.zeros((micro_count, tok_rows, model_width), jnp.bfloat16),
        jnp.zeros((model_width, n_expert), jnp.float32),
        jnp.zeros((model_width,), jnp.float32),
    )
    final = lax.fori_loop(0, ticks, backward_tick, start_bwd)
    _, keep_rows, keep_dy, keep_hidden, keep_dab, stash_grad, acc_router, acc_gain = final
    grad_gu = jnp.einsum(
        "msekd,msekf->edf", keep_rows, keep_dab, preferred_element_type=jnp.float32
    )
    grad_dn = jnp.einsum(
        "msekf,msekd->efd", keep_hidden, keep_dy, preferred_element_type=jnp.float32
    )
    sum_router, sum_gain = (
        lax.psum(acc_router.astype(jnp.bfloat16), ("expert", "dp")).astype(jnp.float32),
        lax.psum(acc_gain.astype(jnp.bfloat16), ("expert", "dp")).astype(jnp.float32),
    )
    first_term = jnp.where(segment_idx == 0, stash_grad.astype(jnp.float32), 0.0)
    grad_in = lax.psum_scatter(
        first_term.astype(jnp.bfloat16), "section", scatter_dimension=2, tiled=True
    )
    return (grad_in, grad_gu[None], grad_dn[None], sum_router[None], sum_gain[None])


def solution(mesh):
    in_specs = (
        P(None, ("expert", "dp"), "section"),
        P(None, ("expert", "dp"), "section"),
        P("section", None, ("expert", "dp"), None),
        P("section", None),
        P("section", None, None),
        P("section", ("expert", "dp"), None, None),
        P("section", ("expert", "dp"), None, None),
    )
    out_specs = (
        P(None, ("expert", "dp"), "section"),
        P("section", ("expert", "dp"), None, None),
        P("section", ("expert", "dp"), None, None),
        P("section", None, None),
        P("section", None),
    )
    return jax.shard_map(local, mesh=mesh, in_specs=in_specs, out_specs=out_specs, check_vma=False)
```

profile of v0, /device:TPU:8, one launch (start us, length us, event | category | flops | bytes accessed | tf_op | source)
XLA Modules:
  0.0 864.4 jit_solution(11679668147466827216)
XLA Ops:
  8.1 10.6 %all_gather.6 = bf16[8,16,2048]{2,1,0:T(8,128)(2,1)} all-gather(bf16[8,16,1024]{2,1,0:T(8,128)(2,1)} %param.12), channel_id=1, replica_groups=mesh['section'=2,'expert'=4,'dp'=4] {'section'}, dimensions={2}, use_global_device_ids=true | all-gather | bytes 786432 | tf_op jit(solution)/shard_map/all_gather | solution.py:85
  18.6 8.9 %all_gather.7 = bf16[8,16,2048]{2,1,0:T(8,128)(2,1)} all-gather(bf16[8,16,1024]{2,1,0:T(8,128)(2,1)} %param.11), channel_id=1, replica_groups=mesh['section'=2,'expert'=4,'dp'=4] {'section'}, dimensions={2}, use_global_device_ids=true | all-gather | bytes 786432 | tf_op jit(solution)/shard_map/all_gather | solution.py:84
  31.9 327.4 %while.48 = (s32[]{:T(128)}, bf16[16,2048]{1,0:T(8,128)(2,1)S(1)}, bf16[8,16,2048]{2,1,0:T(8,128)(2,1)S(1)}, bf16[8,32,2048]{2,1,0:T(8,128)(2,1)}, bf16[8,16,1,2...) while((s32[]{:T(128)}, bf16[16,2048]{1,0:T(8,128)(2,1)S(1)}, ...), condition=%wide.region_7.8_spmd, body=%wide.region_0.7_spmd.sunk | while | flops 209598352 | bytes 11630114 | solution.py:140
  35.7 6.3 all-to-all-start
  52.2 4.8 all-to-all-start.1
  57.8 5.3 all-to-all-done.1
  72.5 4.8 all-to-all-start
  79.6 3.8 all-to-all-done
  87.7 4.8 all-to-all-start.1
  93.3 5.3 all-to-all-done.1
  98.9 4.3 collective-permute-start
  108.9 4.8 all-to-all-start
  115.9 3.8 all-to-all-done
  124.0 4.8 all-to-all-start.1
  129.6 5.3 all-to-all-done.1
  135.2 4.3 collective-permute-start
  145.2 4.8 all-to-all-start
  152.2 3.8 all-to-all-done
  160.3 4.8 all-to-all-start.1
  165.9 5.3 all-to-all-done.1
  171.6 4.3 collective-permute-start
  181.5 4.8 all-to-all-start
  196.6 4.8 all-to-all-start.1
  202.2 5.3 all-to-all-done.1
  207.9 4.3 collective-permute-start
  217.8 4.8 all-to-all-start
  233.0 4.8 all-to-all-start.1
  238.5 5.3 all-to-all-done.1
  244.2 4.3 collective-permute-start
  254.1 4.8 all-to-all-start
  269.3 4.8 all-to-all-start.1
  274.9 5.3 all-to-all-done.1
  280.5 4.3 collective-permute-start
  290.5 4.8 all-to-all-start
  305.6 4.8 all-to-all-start.1
  311.2 5.3 all-to-all-done.1
  316.8 4.3 collective-permute-start
  326.8 4.8 all-to-all-start
  341.9 4.8 all-to-all-start.1
  347.5 5.3 all-to-all-done.1
  353.2 4.3 collective-permute-start
  363.5 403.9 %while.49 = (s32[]{:T(128)}, bf16[16,2048]{1,0:T(8,128)(2,1)S(1)}, bf16[8,16,1,2,2048]{4,3,1,2,0:T(2,128)(2,1)}, bf16[8,16,1,2,512]{4,1,3,2,0:T(8,128)(2,1)}, bf...) while((s32[]{:T(128)}, bf16[16,2048]{1,0:T(8,128)(2,1)S(1)}, ...), condition=%wide.region_18.19_spmd.clone, body=%wide.region_8.18_spmd.clone.sunk | while | flops 361911744 | bytes 17806364 | solution.py:214
  369.7 4.8 all-to-all-start.2
  387.4 6.1 all-to-all-start.3
  404.1 4.2 collective-permute-done.1
  414.5 4.8 all-to-all-start.2
  432.2 6.1 all-to-all-start.3
  459.4 4.8 all-to-all-start.2
  477.1 6.1 all-to-all-start.3
  504.3 4.8 all-to-all-start.2
  522.0 6.1 all-to-all-start.3
  549.2 4.8 all-to-all-start.2
  566.9 6.1 all-to-all-start.3
  594.0 4.8 all-to-all-start.2
  611.7 6.1 all-to-all-start.3
  638.9 4.8 all-to-all-start.2
  656.6 6.1 all-to-all-start.3
  683.8 4.8 all-to-all-start.2
  701.5 6.1 all-to-all-start.3
  728.7 4.8 all-to-all-start.2
  746.4 6.1 all-to-all-start.3
  770.1 6.2 convolution_bitcast_fusion.1
  776.3 32.1 %psum.15 = bf16[1,2048]{1,0:T(2,128)(2,1)S(1)} all-reduce(bf16[1,2048]{1,0:T(2,128)(2,1)S(1)} %broadcast_in_dim.182), channel_id=1, replica_groups=mesh['section'=2,'expert'=4,'dp'=4] {'expert','dp'}, use_global_device_ids=true, to_apply=%region_21.22 | all-reduce | flops 2048 | bytes 8192 | tf_op jit(solution)/shard_map/psum | solution.py:224
  812.1 43.3 %all-reduce.2.cloned.1.call-done = bf16[1,2048,16]{1,2,0:T(8,128)(2,1)} async-done(((bf16[1,2048,16]{1,2,0:T(8,128)(2,1)}), bf16[1,2048,16]{1,2,0:T(8,128)(2,1)}) %all-reduce.2.cloned.1.call-update) | async-done | bytes 65552 | tf_op jit(solution)/shard_map/psum | solution.py:223
  (697 shorter events, 462.8 us)
Async XLA Ops:
  8.0 23.9 %copy-start.2 = (f32[1,2048]{1,0:T(1,128)S(1)}, f32[1,2048]{1,0:T(1,128)}, u32[]{:S(2)}) copy-start(f32[1,2048]{1,0:T(1,128)} %param.14) | copy-start | bytes 24580
  8.0 23.9 %copy-start = (bf16[1,1,512,2048]{3,2,1,0:T(8,128)(2,1)S(1)}, bf16[1,1,512,2048]{3,2,1,0:T(8,128)(2,1)}, u32[]{:S(2)}) copy-start(bf16[1,1,512,2048]{3,2,1,0:T(8,128)(2,1)} %param.17) | copy-start | bytes 6291460
  8.0 847.5 %all-reduce.2.cloned.1.call-start = ((), (), s32[]{:S(2)}) async-start(), calls=%async_computation.6 | async-start | bytes 131072 | tf_op jit(solution)/shard_map/psum | solution.py:223
  35.7 12.3 %all-to-all-start = ((bf16[16,1,2,2048]{3,2,1,0:T(2,128)(2,1)}), bf16[16,1,2,2048]{3,2,1,0:T(2,128)(2,1)S(1)}, u32[]{:S(2)}, u32[]{:S(2)}) async-start(bf16[16,1,2,2048]{3,2,1,0:T(2,128)(2,1)} %bitcast.324), calls=%async_computation | async-start | bytes 262144 | tf_op jit(solution)/shard_map/while/body/eval_jaxpr/all_to_all | solution.py:118
  52.2 10.9 %all-to-all-start.1 = ((bf16[16,1,2,2048]{3,2,1,0:T(2,128)(2,1)}), bf16[16,1,2,2048]{3,2,1,0:T(2,128)(2,1)S(1)}, u32[]{:S(2)}, u32[]{:S(2)}) async-start(bf16[16,1,2,2048]{3,2,1,0:T(2,128)(2,1)} %copy.84), calls=%async_computation.1 | async-start | bytes 262144 | tf_op jit(solution)/shard_map/while/body/eval_jaxpr/all_to_all | solution.py:101
  63.5 5.3 collective-permute-start
  72.5 10.9 %all-to-all-start = ((bf16[16,1,2,2048]{3,2,1,0:T(2,128)(2,1)}), bf16[16,1,2,2048]{3,2,1,0:T(2,128)(2,1)S(1)}, u32[]{:S(2)}, u32[]{:S(2)}) async-start(bf16[16,1,2,2048]{3,2,1,0:T(2,128)(2,1)} %bitcast.324), calls=%async_computation | async-start | bytes 262144 | tf_op jit(solution)/shard_map/while/body/eval_jaxpr/all_to_all | solution.py:118
  87.7 10.9 %all-to-all-start.1 = ((bf16[16,1,2,2048]{3,2,1,0:T(2,128)(2,1)}), bf16[16,1,2,2048]{3,2,1,0:T(2,128)(2,1)S(1)}, u32[]{:S(2)}, u32[]{:S(2)}) async-start(bf16[16,1,2,2048]{3,2,1,0:T(2,128)(2,1)} %copy.84), calls=%async_computation.1 | async-start | bytes 262144 | tf_op jit(solution)/shard_map/while/body/eval_jaxpr/all_to_all | solution.py:101
  98.9 6.2 collective-permute-start
  108.9 10.9 %all-to-all-start = ((bf16[16,1,2,2048]{3,2,1,0:T(2,128)(2,1)}), bf16[16,1,2,2048]{3,2,1,0:T(2,128)(2,1)S(1)}, u32[]{:S(2)}, u32[]{:S(2)}) async-start(bf16[16,1,2,2048]{3,2,1,0:T(2,128)(2,1)} %bitcast.324), calls=%async_computation | async-start | bytes 262144 | tf_op jit(solution)/shard_map/while/body/eval_jaxpr/all_to_all | solution.py:118
  124.0 10.9 %all-to-all-start.1 = ((bf16[16,1,2,2048]{3,2,1,0:T(2,128)(2,1)}), bf16[16,1,2,2048]{3,2,1,0:T(2,128)(2,1)S(1)}, u32[]{:S(2)}, u32[]{:S(2)}) async-start(bf16[16,1,2,2048]{3,2,1,0:T(2,128)(2,1)} %copy.84), calls=%async_computation.1 | async-start | bytes 262144 | tf_op jit(solution)/shard_map/while/body/eval_jaxpr/all_to_all | solution.py:101
  135.2 6.2 collective-permute-start
  145.2 10.9 %all-to-all-start = ((bf16[16,1,2,2048]{3,2,1,0:T(2,128)(2,1)}), bf16[16,1,2,2048]{3,2,1,0:T(2,128)(2,1)S(1)}, u32[]{:S(2)}, u32[]{:S(2)}) async-start(bf16[16,1,2,2048]{3,2,1,0:T(2,128)(2,1)} %bitcast.324), calls=%async_computation | async-start | bytes 262144 | tf_op jit(solution)/shard_map/while/body/eval_jaxpr/all_to_all | solution.py:118
  160.3 10.9 %all-to-all-start.1 = ((bf16[16,1,2,2048]{3,2,1,0:T(2,128)(2,1)}), bf16[16,1,2,2048]{3,2,1,0:T(2,128)(2,1)S(1)}, u32[]{:S(2)}, u32[]{:S(2)}) async-start(bf16[16,1,2,2048]{3,2,1,0:T(2,128)(2,1)} %copy.84), calls=%async_computation.1 | async-start | bytes 262144 | tf_op jit(solution)/shard_map/while/body/eval_jaxpr/all_to_all | solution.py:101
  171.6 6.2 collective-permute-start
  181.5 10.9 %all-to-all-start = ((bf16[16,1,2,2048]{3,2,1,0:T(2,128)(2,1)}), bf16[16,1,2,2048]{3,2,1,0:T(2,128)(2,1)S(1)}, u32[]{:S(2)}, u32[]{:S(2)}) async-start(bf16[16,1,2,2048]{3,2,1,0:T(2,128)(2,1)} %bitcast.324), calls=%async_computation | async-start | bytes 262144 | tf_op jit(solution)/shard_map/while/body/eval_jaxpr/all_to_all | solution.py:118
  196.6 10.9 %all-to-all-start.1 = ((bf16[16,1,2,2048]{3,2,1,0:T(2,128)(2,1)}), bf16[16,1,2,2048]{3,2,1,0:T(2,128)(2,1)S(1)}, u32[]{:S(2)}, u32[]{:S(2)}) async-start(bf16[16,1,2,2048]{3,2,1,0:T(2,128)(2,1)} %copy.84), calls=%async_computation.1 | async-start | bytes 262144 | tf_op jit(solution)/shard_map/while/body/eval_jaxpr/all_to_all | solution.py:101
  207.9 6.2 collective-permute-start
  217.8 10.9 %all-to-all-start = ((bf16[16,1,2,2048]{3,2,1,0:T(2,128)(2,1)}), bf16[16,1,2,2048]{3,2,1,0:T(2,128)(2,1)S(1)}, u32[]{:S(2)}, u32[]{:S(2)}) async-start(bf16[16,1,2,2048]{3,2,1,0:T(2,128)(2,1)} %bitcast.324), calls=%async_computation | async-start | bytes 262144 | tf_op jit(solution)/shard_map/while/body/eval_jaxpr/all_to_all | solution.py:118
  233.0 10.9 %all-to-all-start.1 = ((bf16[16,1,2,2048]{3,2,1,0:T(2,128)(2,1)}), bf16[16,1,2,2048]{3,2,1,0:T(2,128)(2,1)S(1)}, u32[]{:S(2)}, u32[]{:S(2)}) async-start(bf16[16,1,2,2048]{3,2,1,0:T(2,128)(2,1)} %copy.84), calls=%async_computation.1 | async-start | bytes 262144 | tf_op jit(solution)/shard_map/while/body/eval_jaxpr/all_to_all | solution.py:101
  244.2 6.2 collective-permute-start
  254.1 10.9 %all-to-all-start = ((bf16[16,1,2,2048]{3,2,1,0:T(2,128)(2,1)}), bf16[16,1,2,2048]{3,2,1,0:T(2,128)(2,1)S(1)}, u32[]{:S(2)}, u32[]{:S(2)}) async-start(bf16[16,1,2,2048]{3,2,1,0:T(2,128)(2,1)} %bitcast.324), calls=%async_computation | async-start | bytes 262144 | tf_op jit(solution)/shard_map/while/body/eval_jaxpr/all_to_all | solution.py:118
  269.3 10.9 %all-to-all-start.1 = ((bf16[16,1,2,2048]{3,2,1,0:T(2,128)(2,1)}), bf16[16,1,2,2048]{3,2,1,0:T(2,128)(2,1)S(1)}, u32[]{:S(2)}, u32[]{:S(2)}) async-start(bf16[16,1,2,2048]{3,2,1,0:T(2,128)(2,1)} %copy.84), calls=%async_computation.1 | async-start | bytes 262144 | tf_op jit(solution)/shard_map/while/body/eval_jaxpr/all_to_all | solution.py:101
  280.5 6.2 collective-permute-start
  290.5 10.9 %all-to-all-start = ((bf16[16,1,2,2048]{3,2,1,0:T(2,128)(2,1)}), bf16[16,1,2,2048]{3,2,1,0:T(2,128)(2,1)S(1)}, u32[]{:S(2)}, u32[]{:S(2)}) async-start(bf16[16,1,2,2048]{3,2,1,0:T(2,128)(2,1)} %bitcast.324), calls=%async_computation | async-start | bytes 262144 | tf_op jit(solution)/shard_map/while/body/eval_jaxpr/all_to_all | solution.py:118
  305.6 10.9 %all-to-all-start.1 = ((bf16[16,1,2,2048]{3,2,1,0:T(2,128)(2,1)}), bf16[16,1,2,2048]{3,2,1,0:T(2,128)(2,1)S(1)}, u32[]{:S(2)}, u32[]{:S(2)}) async-start(bf16[16,1,2,2048]{3,2,1,0:T(2,128)(2,1)} %copy.84), calls=%async_computation.1 | async-start | bytes 262144 | tf_op jit(solution)/shard_map/while/body/eval_jaxpr/all_to_all | solution.py:101
  316.8 6.2 collective-permute-start
  326.8 10.9 %all-to-all-start = ((bf16[16,1,2,2048]{3,2,1,0:T(2,128)(2,1)}), bf16[16,1,2,2048]{3,2,1,0:T(2,128)(2,1)S(1)}, u32[]{:S(2)}, u32[]{:S(2)}) async-start(bf16[16,1,2,2048]{3,2,1,0:T(2,128)(2,1)} %bitcast.324), calls=%async_computation | async-start | bytes 262144 | tf_op jit(solution)/shard_map/while/body/eval_jaxpr/all_to_all | solution.py:118
  341.9 10.9 %all-to-all-start.1 = ((bf16[16,1,2,2048]{3,2,1,0:T(2,128)(2,1)}), bf16[16,1,2,2048]{3,2,1,0:T(2,128)(2,1)S(1)}, u32[]{:S(2)}, u32[]{:S(2)}) async-start(bf16[16,1,2,2048]{3,2,1,0:T(2,128)(2,1)} %copy.84), calls=%async_computation.1 | async-start | bytes 262144 | tf_op jit(solution)/shard_map/while/body/eval_jaxpr/all_to_all | solution.py:101
  353.2 6.2 collective-permute-start
  369.7 12.5 %all-to-all-start.2 = ((bf16[16,1,2,2048]{3,2,1,0:T(2,128)(2,1)}), bf16[16,1,2,2048]{3,2,1,0:T(2,128)(2,1)S(1)}, u32[]{:S(2)}, u32[]{:S(2)}) async-start(bf16[16,1,2,2048]{3,2,1,0:T(2,128)(2,1)} %bitcast.359), calls=%async_computation.2 | async-start | bytes 262144 | tf_op jit(solution)/shard_map/while/body/eval_jaxpr/all_to_all | solution.py:162
  387.4 12.0 %all-to-all-start.3 = ((bf16[16,1,2,2048]{3,2,1,0:T(2,128)(2,1)}), bf16[16,1,2,2048]{3,2,1,0:T(2,128)(2,1)S(1)}, u32[]{:S(2)}, u32[]{:S(2)}) async-start(bf16[16,1,2,2048]{3,2,1,0:T(2,128)(2,1)} %copy.87), calls=%async_computation.3 | async-start | bytes 262144 | tf_op jit(solution)/shard_map/while/body/eval_jaxpr/all_to_all | solution.py:167
  402.2 6.1 collective-permute-start.1
  414.5 12.6 %all-to-all-start.2 = ((bf16[16,1,2,2048]{3,2,1,0:T(2,128)(2,1)}), bf16[16,1,2,2048]{3,2,1,0:T(2,128)(2,1)S(1)}, u32[]{:S(2)}, u32[]{:S(2)}) async-start(bf16[16,1,2,2048]{3,2,1,0:T(2,128)(2,1)} %bitcast.359), calls=%async_computation.2 | async-start | bytes 262144 | tf_op jit(solution)/shard_map/while/body/eval_jaxpr/all_to_all | solution.py:162
  432.2 12.0 %all-to-all-start.3 = ((bf16[16,1,2,2048]{3,2,1,0:T(2,128)(2,1)}), bf16[16,1,2,2048]{3,2,1,0:T(2,128)(2,1)S(1)}, u32[]{:S(2)}, u32[]{:S(2)}) async-start(bf16[16,1,2,2048]{3,2,1,0:T(2,128)(2,1)} %copy.87), calls=%async_computation.3 | async-start | bytes 262144 | tf_op jit(solution)/shard_map/while/body/eval_jaxpr/all_to_all | solution.py:167
  447.1 6.1 collective-permute-start.1
  453.3 18.3 %copy-start.7 = (f32[16]{0:T(128)}, f32[16]{0:T(128)S(1)}, u32[]{:S(2)}) copy-start(f32[16]{0:T(128)S(1)} %add_rsqrt_fusion.5) | copy-start | bytes 196 | tf_op jit(solution)/shard_map/while
  459.4 12.6 %all-to-all-start.2 = ((bf16[16,1,2,2048]{3,2,1,0:T(2,128)(2,1)}), bf16[16,1,2,2048]{3,2,1,0:T(2,128)(2,1)S(1)}, u32[]{:S(2)}, u32[]{:S(2)}) async-start(bf16[16,1,2,2048]{3,2,1,0:T(2,128)(2,1)} %bitcast.359), calls=%async_computation.2 | async-start | bytes 262144 | tf_op jit(solution)/shard_map/while/body/eval_jaxpr/all_to_all | solution.py:162
  477.1 12.0 %all-to-all-start.3 = ((bf16[16,1,2,2048]{3,2,1,0:T(2,128)(2,1)}), bf16[16,1,2,2048]{3,2,1,0:T(2,128)(2,1)S(1)}, u32[]{:S(2)}, u32[]{:S(2)}) async-start(bf16[16,1,2,2048]{3,2,1,0:T(2,128)(2,1)} %copy.87), calls=%async_computation.3 | async-start | bytes 262144 | tf_op jit(solution)/shard_map/while/body/eval_jaxpr/all_to_all | solution.py:167
  491.9 6.1 collective-permute-start.1
  504.3 12.6 %all-to-all-start.2 = ((bf16[16,1,2,2048]{3,2,1,0:T(2,128)(2,1)}), bf16[16,1,2,2048]{3,2,1,0:T(2,128)(2,1)S(1)}, u32[]{:S(2)}, u32[]{:S(2)}) async-start(bf16[16,1,2,2048]{3,2,1,0:T(2,128)(2,1)} %bitcast.359), calls=%async_computation.2 | async-start | bytes 262144 | tf_op jit(solution)/shard_map/while/body/eval_jaxpr/all_to_all | solution.py:162
  522.0 12.0 %all-to-all-start.3 = ((bf16[16,1,2,2048]{3,2,1,0:T(2,128)(2,1)}), bf16[16,1,2,2048]{3,2,1,0:T(2,128)(2,1)S(1)}, u32[]{:S(2)}, u32[]{:S(2)}) async-start(bf16[16,1,2,2048]{3,2,1,0:T(2,128)(2,1)} %copy.87), calls=%async_computation.3 | async-start | bytes 262144 | tf_op jit(solution)/shard_map/while/body/eval_jaxpr/all_to_all | solution.py:167
  536.8 6.1 collective-permute-start.1
  543.1 18.3 %copy-start.7 = (f32[16]{0:T(128)}, f32[16]{0:T(128)S(1)}, u32[]{:S(2)}) copy-start(f32[16]{0:T(128)S(1)} %add_rsqrt_fusion.5) | copy-start | bytes 196 | tf_op jit(solution)/shard_map/while
  549.2 12.6 %all-to-all-start.2 = ((bf16[16,1,2,2048]{3,2,1,0:T(2,128)(2,1)}), bf16[16,1,2,2048]{3,2,1,0:T(2,128)(2,1)S(1)}, u32[]{:S(2)}, u32[]{:S(2)}) async-start(bf16[16,1,2,2048]{3,2,1,0:T(2,128)(2,1)} %bitcast.359), calls=%async_computation.2 | async-start | bytes 262144 | tf_op jit(solution)/shard_map/while/body/eval_jaxpr/all_to_all | solution.py:162
  566.9 12.0 %all-to-all-start.3 = ((bf16[16,1,2,2048]{3,2,1,0:T(2,128)(2,1)}), bf16[16,1,2,2048]{3,2,1,0:T(2,128)(2,1)S(1)}, u32[]{:S(2)}, u32[]{:S(2)}) async-start(bf16[16,1,2,2048]{3,2,1,0:T(2,128)(2,1)} %copy.87), calls=%async_computation.3 | async-start | bytes 262144 | tf_op jit(solution)/shard_map/while/body/eval_jaxpr/all_to_all | solution.py:167
  581.7 6.1 collective-permute-start.1
  594.0 12.6 %all-to-all-start.2 = ((bf16[16,1,2,2048]{3,2,1,0:T(2,128)(2,1)}), bf16[16,1,2,2048]{3,2,1,0:T(2,128)(2,1)S(1)}, u32[]{:S(2)}, u32[]{:S(2)}) async-start(bf16[16,1,2,2048]{3,2,1,0:T(2,128)(2,1)} %bitcast.359), calls=%async_computation.2 | async-start | bytes 262144 | tf_op jit(solution)/shard_map/while/body/eval_jaxpr/all_to_all | solution.py:162
  611.7 12.0 %all-to-all-start.3 = ((bf16[16,1,2,2048]{3,2,1,0:T(2,128)(2,1)}), bf16[16,1,2,2048]{3,2,1,0:T(2,128)(2,1)S(1)}, u32[]{:S(2)}, u32[]{:S(2)}) async-start(bf16[16,1,2,2048]{3,2,1,0:T(2,128)(2,1)} %copy.87), calls=%async_computation.3 | async-start | bytes 262144 | tf_op jit(solution)/shard_map/while/body/eval_jaxpr/all_to_all | solution.py:167
  626.5 6.1 collective-permute-start.1
  632.8 18.3 %copy-start.7 = (f32[16]{0:T(128)}, f32[16]{0:T(128)S(1)}, u32[]{:S(2)}) copy-start(f32[16]{0:T(128)S(1)} %add_rsqrt_fusion.5) | copy-start | bytes 196 | tf_op jit(solution)/shard_map/while
  638.9 12.6 %all-to-all-start.2 = ((bf16[16,1,2,2048]{3,2,1,0:T(2,128)(2,1)}), bf16[16,1,2,2048]{3,2,1,0:T(2,128)(2,1)S(1)}, u32[]{:S(2)}, u32[]{:S(2)}) async-start(bf16[16,1,2,2048]{3,2,1,0:T(2,128)(2,1)} %bitcast.359), calls=%async_computation.2 | async-start | bytes 262144 | tf_op jit(solution)/shard_map/while/body/eval_jaxpr/all_to_all | solution.py:162
  656.6 12.0 %all-to-all-start.3 = ((bf16[16,1,2,2048]{3,2,1,0:T(2,128)(2,1)}), bf16[16,1,2,2048]{3,2,1,0:T(2,128)(2,1)S(1)}, u32[]{:S(2)}, u32[]{:S(2)}) async-start(bf16[16,1,2,2048]{3,2,1,0:T(2,128)(2,1)} %copy.87), calls=%async_computation.3 | async-start | bytes 262144 | tf_op jit(solution)/shard_map/while/body/eval_jaxpr/all_to_all | solution.py:167
  671.4 6.1 collective-permute-start.1
  677.7 18.3 %copy-start.7 = (f32[16]{0:T(128)}, f32[16]{0:T(128)S(1)}, u32[]{:S(2)}) copy-start(f32[16]{0:T(128)S(1)} %add_rsqrt_fusion.5) | copy-start | bytes 196 | tf_op jit(solution)/shard_map/while
  683.8 12.6 %all-to-all-start.2 = ((bf16[16,1,2,2048]{3,2,1,0:T(2,128)(2,1)}), bf16[16,1,2,2048]{3,2,1,0:T(2,128)(2,1)S(1)}, u32[]{:S(2)}, u32[]{:S(2)}) async-start(bf16[16,1,2,2048]{3,2,1,0:T(2,128)(2,1)} %bitcast.359), calls=%async_computation.2 | async-start | bytes 262144 | tf_op jit(solution)/shard_map/while/body/eval_jaxpr/all_to_all | solution.py:162
  701.5 12.0 %all-to-all-start.3 = ((bf16[16,1,2,2048]{3,2,1,0:T(2,128)(2,1)}), bf16[16,1,2,2048]{3,2,1,0:T(2,128)(2,1)S(1)}, u32[]{:S(2)}, u32[]{:S(2)}) async-start(bf16[16,1,2,2048]{3,2,1,0:T(2,128)(2,1)} %copy.87), calls=%async_computation.3 | async-start | bytes 262144 | tf_op jit(solution)/shard_map/while/body/eval_jaxpr/all_to_all | solution.py:167
  716.3 6.1 collective-permute-start.1
  728.7 12.6 %all-to-all-start.2 = ((bf16[16,1,2,2048]{3,2,1,0:T(2,128)(2,1)}), bf16[16,1,2,2048]{3,2,1,0:T(2,128)(2,1)S(1)}, u32[]{:S(2)}, u32[]{:S(2)}) async-start(bf16[16,1,2,2048]{3,2,1,0:T(2,128)(2,1)} %bitcast.359), calls=%async_computation.2 | async-start | bytes 262144 | tf_op jit(solution)/shard_map/while/body/eval_jaxpr/all_to_all | solution.py:162
  746.4 12.0 %all-to-all-start.3 = ((bf16[16,1,2,2048]{3,2,1,0:T(2,128)(2,1)}), bf16[16,1,2,2048]{3,2,1,0:T(2,128)(2,1)S(1)}, u32[]{:S(2)}, u32[]{:S(2)}) async-start(bf16[16,1,2,2048]{3,2,1,0:T(2,128)(2,1)} %copy.87), calls=%async_computation.3 | async-start | bytes 262144 | tf_op jit(solution)/shard_map/while/body/eval_jaxpr/all_to_all | solution.py:167
  761.2 6.1 collective-permute-start.1
  768.0 89.0 %reduce-scatter.2.cloned.1.call-start = ((), (), s32[]{:S(2)}) async-start(), calls=%async_computation.5 | async-start | bytes 786432 | tf_op jit(solution)/shard_map/reduce_scatter | solution.py:227
  770.1 39.0 %copy-start.3 = (bf16[8,16,1,2,2048]{4,3,1,2,0:T(2,128)(2,1)S(1)}, bf16[8,16,1,2,2048]{4,3,1,2,0:T(2,128)(2,1)}, u32[]{:S(2)}) copy-start(bf16[8,16,1,2,2048]{4,3,1,2,0:T(2,128)(2,1)} %get-tuple-element.697) | copy-start | bytes 3145732
  770.1 39.0 %copy-start.5 = (bf16[8,16,1,2,512]{4,1,3,2,0:T(8,128)(2,1)S(1)}, bf16[8,16,1,2,512]{4,1,3,2,0:T(8,128)(2,1)}, u32[]{:S(2)}) copy-start(bf16[8,16,1,2,512]{4,1,3,2,0:T(8,128)(2,1)} %get-tuple-element.696) | copy-start | bytes 786436
  (24 other events, 323.2 us)
Sparse Core Ops, SparseCore 0:
  768.1 87.3 all-reduce.1
Sparse Core Ops, SparseCore 1:
  771.3 13.1 reduce-scatter.1
where the time goes:
time: 874 us; the launch traced here: 864 us
  starting transfers between devices  235 us (27%)
  waiting for transfers between devices  194 us (22%)
  matrix products  157 us (18%)
  other arithmetic  119 us (14%)
  local copies, waits for them, and re-layouts  90.7 us (10%)
  blocking collectives  51.6 us (6%)
  between operations  15.6 us (2%)
    dynamic_update_slice x63, other arithmetic, keep_row(): lax.dynamic_update_index_in_dim(stash, jnp.where(active, value, old_row),...  67.9 us
    all_to_all x9, starting transfers between devices, backward_tick(): lax.all_to_all(rows_grad, ('expert', 'dp'), split_axis=0, concat_axis=0,...  54.7 us
    dot_general x18, matrix products, expert_inner(): jnp.einsum('sekd,edf->sekf', exp_rows, w_gu, preferred_element_type=jnp.f...  54.1 us
    ppermute x18, starting transfers between devices, shifted(): lax.ppermute(value, axis, [(source, source + steps) for source in range(l...  49.1 us
    all_to_all x9, waiting for transfers between devices, expert_forward(): lax.all_to_all(out_rows, ('expert', 'dp'), split_axis=0, concat_axis=0, t...  47.7 us
    all_to_all x9, starting transfers between devices, forward_tick(): lax.all_to_all(send_rows, ('expert', 'dp'), split_axis=0, concat_axis=0,...  44.6 us
    psum x1, waiting for transfers between devices, local(): lax.psum(acc_router.astype(jnp.bfloat16), ('expert', 'dp'))  43.3 us
    all_to_all x9, starting transfers between devices, backward_tick(): lax.all_to_all(dy_send, ('expert', 'dp'), split_axis=0, concat_axis=0, ti...  43.3 us
  transfers between devices with their start and end apart: 56, of which 46 were waited for; matrix products, arithmetic and copies ran while one was open for 18% of the time, Pallas kernels for 0%

commit v1 on v0

--- a/solution.py
+++ b/solution.py
@@ -4,6 +4,20 @@
 from jax.sharding import PartitionSpec as P
 
 EPS = 1e-05
+
+
+def cut_edges(target, join_dim, q_in):
+    all_values, formed = (target.shape[:join_dim], target.shape[join_dim + 1 :])
+    p_next = target.reshape(*all_values, q_in, -1, *formed)
+    return jnp.moveaxis(p_next, join_dim, 0)
+
+
+def _clear_ways(z_in, row_dim):
+    z_in = jnp.moveaxis(z_in, 0, row_dim)
+    t_next = z_in.shape
+    return z_in.reshape(
+        *t_next[:row_dim], t_next[row_dim] * t_next[row_dim + 1], *t_next[row_dim + 2 :]
+    )
 
 
 def shifted(value, axis, steps):
@@ -114,8 +128,25 @@
         expert_hits, slot_place = slot_tables(route_rows, n_expert, capacity)
         send_rows = jnp.einsum("ktc,td->cd", slot_place, normed, preferred_element_type=jnp.float32)
         send_rows = send_rows.astype(jnp.bfloat16).reshape(rows_shape)
+
+        def deliver_field_over_axis(frame, shard_axis, unit, xs):
+            part_now = lax.axis_size(shard_axis)
+            side_arr = lax.axis_index(shard_axis)
+            vec_out, outcome_arr = (part_now, side_arr)
+            z2 = cut_edges(frame, unit, vec_out)
+            log = [z2[outcome_arr]]
+            for p in range(1, vec_out):
+                finding = z2[outcome_arr ^ p]
+                local_next = lax.ppermute(
+                    finding, shard_axis, [(rr, rr ^ p) for rr in range(vec_out)]
+                )
+                log.append(local_next)
+            x_next = jnp.stack(log)
+            z2 = x_next[outcome_arr ^ jnp.arange(vec_out)]
+            return _clear_ways(z2, xs)
+
         returned, landed = expert_forward(
-            lax.all_to_all(send_rows, ("expert", "dp"), split_axis=0, concat_axis=0, tiled=True)
+            deliver_field_over_axis(send_rows, ("expert", "dp"), 0, 0)
         )
         back_flat = returned.reshape(cells, model_width)
         picked = jnp.einsum(

time: 874 us -> 1020 us (1.17)
  starting transfers between devices: 235 us -> 389 us
    ppermute x0 -> x135, starting transfers between devices: none -> 177 us  [deliver_field_over_axis(): lax.ppermute(finding, shard_axis, [(rr, rr ^ p) for rr in range(vec_out)])]
    all_to_all x9 -> x0, starting transfers between devices: 44.6 us -> none  [forward_tick(): lax.all_to_all(send_rows, ('expert', 'dp'), split_axis=0, concat_axis=0,...]
    all_to_all x9 -> x0, waiting for transfers between devices: 34.5 us -> none  [forward_tick(): lax.all_to_all(send_rows, ('expert', 'dp'), split_axis=0, concat_axis=0,...]
    ppermute x0 -> x135, waiting for transfers between devices: none -> 33.9 us  [deliver_field_over_axis(): lax.ppermute(finding, shard_axis, [(rr, rr ^ p) for rr in range(vec_out)])]
    all_to_all x9, starting transfers between devices: 43.1 us -> 64.6 us  [expert_forward(): lax.all_to_all(out_rows, ('expert', 'dp'), split_axis=0, concat_axis=0, t...]
    dynamic_slice x45 -> x36, local copies, waits for them, and re-layouts: 32.7 us -> 23.6 us  [keep_row(): old_row = lax.dynamic_index_in_dim(stash, position, 0, keepdims=False)]
  transfers between devices with their start and end apart: 56 -> 182, of which waited for: 46 -> 55; matrix products, arithmetic and copies ran while one was open for 18% -> 16% of each run, Pallas kernels for 0% -> 0%
where the time goes in v1:
time: 1020 us
  starting transfers between devices  389 us (38%)
  waiting for transfers between devices  184 us (18%)
  matrix products  157 us (15%)
  other arithmetic  128 us (13%)
  local copies, waits for them, and re-layouts  86.4 us (8%)
  blocking collectives  51.6 us (5%)
  between operations  15.6 us (2%)
    ppermute x135, starting transfers between devices, deliver_field_over_axis(): lax.ppermute(finding, shard_axis, [(rr, rr ^ p) for rr in range(vec_out)])  177 us
    dynamic_update_slice x63, other arithmetic, keep_row(): lax.dynamic_update_index_in_dim(stash, jnp.where(active, value, old_row),...  76 us
    all_to_all x9, starting transfers between devices, expert_forward(): lax.all_to_all(out_rows, ('expert', 'dp'), split_axis=0, concat_axis=0, t...  64.6 us
    all_to_all x9, starting transfers between devices, backward_tick(): lax.all_to_all(rows_grad, ('expert', 'dp'), split_axis=0, concat_axis=0,...  54.7 us
    dot_general x18, matrix products, expert_inner(): jnp.einsum('sekd,edf->sekf', exp_rows, w_gu, preferred_element_type=jnp.f...  54.2 us
    ppermute x18, starting transfers between devices, shifted(): lax.ppermute(value, axis, [(source, source + steps) for source in range(l...  49.1 us
    all_to_all x9, starting transfers between devices, backward_tick(): lax.all_to_all(dy_send, ('expert', 'dp'), split_axis=0, concat_axis=0, ti...  43.3 us
    psum x1, waiting for transfers between devices, local(): lax.psum(acc_router.astype(jnp.bfloat16), ('expert', 'dp'))  43.2 us
  transfers between devices with their start and end apart: 182, of which 55 were waited for; matrix products, arithmetic and copies ran while one was open for 16% of the time, Pallas kernels for 0%

profile of v1, /device:TPU:8, one launch (start us, length us, event | category | flops | bytes accessed | tf_op | source)
XLA Modules:
  0.0 1015.4 jit_solution(10446950949976263124)
XLA Ops:
  8.1 10.6 %all_gather.6 = bf16[8,16,2048]{2,1,0:T(8,128)(2,1)} all-gather(bf16[8,16,1024]{2,1,0:T(8,128)(2,1)} %param.12), channel_id=1, replica_groups=mesh['section'=2,'expert'=4,'dp'=4] {'section'}, dimensions={2}, use_global_device_ids=true | all-gather | bytes 786432 | tf_op jit(solution)/shard_map/all_gather | solution.py:99
  18.6 8.9 all_gather.7
  31.9 478.4 %while.48 = (s32[]{:T(128)}, bf16[16,2048]{1,0:T(8,128)(2,1)S(1)}, bf16[8,16,2048]{2,1,0:T(8,128)(2,1)S(1)}, bf16[8,32,2048]{2,1,0:T(8,128)(2,1)}, bf16[8,16,1,2...) while((s32[]{:T(128)}, bf16[16,2048]{1,0:T(8,128)(2,1)S(1)}, ...), condition=%wide.region_7.8_spmd, body=%wide.region_0.7_spmd.sunk | while | flops 209599520 | bytes 12242162 | solution.py:171
  65.7 6.6 all-to-all-start
  74.0 4.4 all-to-all-done
  102.7 4.7 collective-permute-start.12
  117.5 7.3 all-to-all-start
  126.5 4.3 all-to-all-done
  131.1 4.3 collective-permute-start.15
  156.0 4.7 collective-permute-start.12
  170.8 7.3 all-to-all-start
  179.8 4.3 all-to-all-done
  184.4 4.3 collective-permute-start.15
  209.3 4.7 collective-permute-start.12
  224.1 7.3 all-to-all-start
  233.0 4.3 all-to-all-done
  237.7 4.3 collective-permute-start.15
  262.6 4.7 collective-permute-start.12
  277.4 7.3 all-to-all-start
  286.3 4.3 all-to-all-done
  291.0 4.3 collective-permute-start.15
  315.9 4.7 collective-permute-start.12
  330.7 7.3 all-to-all-start
  339.6 4.3 all-to-all-done
  344.3 4.3 collective-permute-start.15
  369.2 4.7 collective-permute-start.12
  384.0 7.3 all-to-all-start
  392.9 4.3 all-to-all-done
  397.5 4.3 collective-permute-start.15
  422.5 4.7 collective-permute-start.12
  437.2 7.3 all-to-all-start
  446.2 4.3 all-to-all-done
  450.8 4.3 collective-permute-start.15
  475.8 4.7 collective-permute-start.12
  490.5 7.3 all-to-all-start
  499.5 4.3 all-to-all-done
  504.1 4.3 collective-permute-start.15
  514.4 403.9 %while.49 = (s32[]{:T(128)}, bf16[16,2048]{1,0:T(8,128)(2,1)S(1)}, bf16[8,16,1,2,2048]{4,3,1,2,0:T(2,128)(2,1)}, bf16[8,16,1,2,512]{4,1,3,2,0:T(8,128)(2,1)}, bf...) while((s32[]{:T(128)}, bf16[16,2048]{1,0:T(8,128)(2,1)S(1)}, ...), condition=%wide.region_18.19_spmd.clone, body=%wide.region_8.18_spmd.clone.sunk | while | flops 361911744 | bytes 17806364 | solution.py:245
  520.6 4.8 all-to-all-start.1
  538.3 6.1 all-to-all-start.2
  546.7 3.7 all-to-all-done.2
  555.1 4.2 collective-permute-done.16
  565.5 4.8 all-to-all-start.1
  583.2 6.1 all-to-all-start.2
  591.6 3.7 all-to-all-done.2
  610.4 4.8 all-to-all-start.1
  628.1 6.1 all-to-all-start.2
  655.3 4.8 all-to-all-start.1
  673.0 6.1 all-to-all-start.2
  681.3 3.7 all-to-all-done.2
  700.1 4.8 all-to-all-start.1
  717.8 6.1 all-to-all-start.2
  745.0 4.8 all-to-all-start.1
  762.7 6.1 all-to-all-start.2
  789.9 4.8 all-to-all-start.1
  807.6 6.1 all-to-all-start.2
  815.9 3.7 all-to-all-done.2
  834.8 4.8 all-to-all-start.1
  852.5 6.1 all-to-all-start.2
  879.7 4.8 all-to-all-start.1
  897.3 6.1 all-to-all-start.2
  921.2 6.2 convolution_bitcast_fusion.1
  927.5 32.1 %psum.15 = bf16[1,2048]{1,0:T(2,128)(2,1)S(1)} all-reduce(bf16[1,2048]{1,0:T(2,128)(2,1)S(1)} %broadcast_in_dim.180), channel_id=1, replica_groups=mesh['section'=2,'expert'=4,'dp'=4] {'expert','dp'}, use_global_device_ids=true, to_apply=%region_21.22 | all-reduce | flops 2048 | bytes 8192 | tf_op jit(solution)/shard_map/psum | solution.py:255
  963.2 43.2 %all-reduce.2.cloned.1.call-done = bf16[1,2048,16]{1,2,0:T(8,128)(2,1)} async-done(((bf16[1,2048,16]{1,2,0:T(8,128)(2,1)}), bf16[1,2048,16]{1,2,0:T(8,128)(2,1)}) %all-reduce.2.cloned.1.call-update) | async-done | bytes 65552 | tf_op jit(solution)/shard_map/psum | solution.py:254
  (1111 shorter events, 603.0 us)
Async XLA Ops:
  8.0 998.4 %all-reduce.2.cloned.1.call-start = ((), (), s32[]{:S(2)}) async-start(), calls=%async_computation.5 | async-start | bytes 131072 | tf_op jit(solution)/shard_map/psum | solution.py:254
  35.4 8.4 collective-permute-start.1
  38.9 8.4 collective-permute-start.4
  41.4 8.4 collective-permute-start.5
  45.7 8.5 collective-permute-start.8
  47.3 9.3 collective-permute-start.9
  65.7 12.6 %all-to-all-start = ((bf16[16,1,2,2048]{3,2,1,0:T(2,128)(2,1)}), bf16[16,1,2,2048]{3,2,1,0:T(2,128)(2,1)S(1)}, u32[]{:S(2)}, u32[]{:S(2)}) async-start(bf16[16,1,2,2048]{3,2,1,0:T(2,128)(2,1)} %copy.81), calls=%async_computation | async-start | bytes 262144 | tf_op jit(solution)/shard_map/while/body/eval_jaxpr/all_to_all | solution.py:115
  90.9 9.7 collective-permute-start.4
  96.9 10.5 %collective-permute-start.8 = (bf16[1,1,2,2048]{3,2,1,0:T(2,128)(2,1)S(1)}, bf16[1,1,2,2048]{3,2,1,0:T(2,128)(2,1)S(1)}, u32[]{:S(2)}, u32[]{:S(2)}) collective-permute-start(bf16[1,1,2,2048]{3,2,1,0:T(2,128)(2,1)S(1)} %get-tuple-element.1152), channel_id=1, source_target_pairs={{0,9},{1,8},{2,11},{3,10},{4,13},{5,12},{6,15},{7,14},{8,1},{9,0},... | collective-permute-start | bytes 24584 | tf_op jit(solution)/shard_map/while/body/eval_jaxpr/ppermute | solution.py:140
  100.7 7.8 collective-permute-start.10
  117.5 13.2 %all-to-all-start = ((bf16[16,1,2,2048]{3,2,1,0:T(2,128)(2,1)}), bf16[16,1,2,2048]{3,2,1,0:T(2,128)(2,1)S(1)}, u32[]{:S(2)}, u32[]{:S(2)}) async-start(bf16[16,1,2,2048]{3,2,1,0:T(2,128)(2,1)} %copy.81), calls=%async_computation | async-start | bytes 262144 | tf_op jit(solution)/shard_map/while/body/eval_jaxpr/all_to_all | solution.py:115
  144.2 9.7 collective-permute-start.4
  148.1 7.8 collective-permute-start.6
  150.2 10.5 %collective-permute-start.8 = (bf16[1,1,2,2048]{3,2,1,0:T(2,128)(2,1)S(1)}, bf16[1,1,2,2048]{3,2,1,0:T(2,128)(2,1)S(1)}, u32[]{:S(2)}, u32[]{:S(2)}) collective-permute-start(bf16[1,1,2,2048]{3,2,1,0:T(2,128)(2,1)S(1)} %get-tuple-element.1152), channel_id=1, source_target_pairs={{0,9},{1,8},{2,11},{3,10},{4,13},{5,12},{6,15},{7,14},{8,1},{9,0},... | collective-permute-start | bytes 24584 | tf_op jit(solution)/shard_map/while/body/eval_jaxpr/ppermute | solution.py:140
  154.0 7.8 collective-permute-start.10
  170.8 13.2 %all-to-all-start = ((bf16[16,1,2,2048]{3,2,1,0:T(2,128)(2,1)}), bf16[16,1,2,2048]{3,2,1,0:T(2,128)(2,1)S(1)}, u32[]{:S(2)}, u32[]{:S(2)}) async-start(bf16[16,1,2,2048]{3,2,1,0:T(2,128)(2,1)} %copy.81), calls=%async_computation | async-start | bytes 262144 | tf_op jit(solution)/shard_map/while/body/eval_jaxpr/all_to_all | solution.py:115
  197.5 9.7 collective-permute-start.4
  201.4 7.8 collective-permute-start.6
  203.5 10.5 %collective-permute-start.8 = (bf16[1,1,2,2048]{3,2,1,0:T(2,128)(2,1)S(1)}, bf16[1,1,2,2048]{3,2,1,0:T(2,128)(2,1)S(1)}, u32[]{:S(2)}, u32[]{:S(2)}) collective-permute-start(bf16[1,1,2,2048]{3,2,1,0:T(2,128)(2,1)S(1)} %get-tuple-element.1152), channel_id=1, source_target_pairs={{0,9},{1,8},{2,11},{3,10},{4,13},{5,12},{6,15},{7,14},{8,1},{9,0},... | collective-permute-start | bytes 24584 | tf_op jit(solution)/shard_map/while/body/eval_jaxpr/ppermute | solution.py:140
  207.3 7.8 collective-permute-start.10
  224.1 13.2 %all-to-all-start = ((bf16[16,1,2,2048]{3,2,1,0:T(2,128)(2,1)}), bf16[16,1,2,2048]{3,2,1,0:T(2,128)(2,1)S(1)}, u32[]{:S(2)}, u32[]{:S(2)}) async-start(bf16[16,1,2,2048]{3,2,1,0:T(2,128)(2,1)} %copy.81), calls=%async_computation | async-start | bytes 262144 | tf_op jit(solution)/shard_map/while/body/eval_jaxpr/all_to_all | solution.py:115
  250.8 9.7 collective-permute-start.4
  254.7 7.8 collective-permute-start.6
  256.8 10.5 %collective-permute-start.8 = (bf16[1,1,2,2048]{3,2,1,0:T(2,128)(2,1)S(1)}, bf16[1,1,2,2048]{3,2,1,0:T(2,128)(2,1)S(1)}, u32[]{:S(2)}, u32[]{:S(2)}) collective-permute-start(bf16[1,1,2,2048]{3,2,1,0:T(2,128)(2,1)S(1)} %get-tuple-element.1152), channel_id=1, source_target_pairs={{0,9},{1,8},{2,11},{3,10},{4,13},{5,12},{6,15},{7,14},{8,1},{9,0},... | collective-permute-start | bytes 24584 | tf_op jit(solution)/shard_map/while/body/eval_jaxpr/ppermute | solution.py:140
  260.6 7.8 collective-permute-start.10
  277.4 13.2 %all-to-all-start = ((bf16[16,1,2,2048]{3,2,1,0:T(2,128)(2,1)}), bf16[16,1,2,2048]{3,2,1,0:T(2,128)(2,1)S(1)}, u32[]{:S(2)}, u32[]{:S(2)}) async-start(bf16[16,1,2,2048]{3,2,1,0:T(2,128)(2,1)} %copy.81), calls=%async_computation | async-start | bytes 262144 | tf_op jit(solution)/shard_map/while/body/eval_jaxpr/all_to_all | solution.py:115
  304.1 9.7 collective-permute-start.4
  308.0 7.8 collective-permute-start.6
  310.1 10.5 %collective-permute-start.8 = (bf16[1,1,2,2048]{3,2,1,0:T(2,128)(2,1)S(1)}, bf16[1,1,2,2048]{3,2,1,0:T(2,128)(2,1)S(1)}, u32[]{:S(2)}, u32[]{:S(2)}) collective-permute-start(bf16[1,1,2,2048]{3,2,1,0:T(2,128)(2,1)S(1)} %get-tuple-element.1152), channel_id=1, source_target_pairs={{0,9},{1,8},{2,11},{3,10},{4,13},{5,12},{6,15},{7,14},{8,1},{9,0},... | collective-permute-start | bytes 24584 | tf_op jit(solution)/shard_map/while/body/eval_jaxpr/ppermute | solution.py:140
  313.9 7.8 collective-permute-start.10
  330.7 13.2 %all-to-all-start = ((bf16[16,1,2,2048]{3,2,1,0:T(2,128)(2,1)}), bf16[16,1,2,2048]{3,2,1,0:T(2,128)(2,1)S(1)}, u32[]{:S(2)}, u32[]{:S(2)}) async-start(bf16[16,1,2,2048]{3,2,1,0:T(2,128)(2,1)} %copy.81), calls=%async_computation | async-start | bytes 262144 | tf_op jit(solution)/shard_map/while/body/eval_jaxpr/all_to_all | solution.py:115
  357.3 9.7 collective-permute-start.4
  361.2 7.8 collective-permute-start.6
  363.4 10.5 %collective-permute-start.8 = (bf16[1,1,2,2048]{3,2,1,0:T(2,128)(2,1)S(1)}, bf16[1,1,2,2048]{3,2,1,0:T(2,128)(2,1)S(1)}, u32[]{:S(2)}, u32[]{:S(2)}) collective-permute-start(bf16[1,1,2,2048]{3,2,1,0:T(2,128)(2,1)S(1)} %get-tuple-element.1152), channel_id=1, source_target_pairs={{0,9},{1,8},{2,11},{3,10},{4,13},{5,12},{6,15},{7,14},{8,1},{9,0},... | collective-permute-start | bytes 24584 | tf_op jit(solution)/shard_map/while/body/eval_jaxpr/ppermute | solution.py:140
  367.2 7.8 collective-permute-start.10
  384.0 13.2 %all-to-all-start = ((bf16[16,1,2,2048]{3,2,1,0:T(2,128)(2,1)}), bf16[16,1,2,2048]{3,2,1,0:T(2,128)(2,1)S(1)}, u32[]{:S(2)}, u32[]{:S(2)}) async-start(bf16[16,1,2,2048]{3,2,1,0:T(2,128)(2,1)} %copy.81), calls=%async_computation | async-start | bytes 262144 | tf_op jit(solution)/shard_map/while/body/eval_jaxpr/all_to_all | solution.py:115
  410.6 9.7 collective-permute-start.4
  414.5 7.8 collective-permute-start.6
  416.7 10.5 %collective-permute-start.8 = (bf16[1,1,2,2048]{3,2,1,0:T(2,128)(2,1)S(1)}, bf16[1,1,2,2048]{3,2,1,0:T(2,128)(2,1)S(1)}, u32[]{:S(2)}, u32[]{:S(2)}) collective-permute-start(bf16[1,1,2,2048]{3,2,1,0:T(2,128)(2,1)S(1)} %get-tuple-element.1152), channel_id=1, source_target_pairs={{0,9},{1,8},{2,11},{3,10},{4,13},{5,12},{6,15},{7,14},{8,1},{9,0},... | collective-permute-start | bytes 24584 | tf_op jit(solution)/shard_map/while/body/eval_jaxpr/ppermute | solution.py:140
  420.5 7.8 collective-permute-start.10
  437.2 13.2 %all-to-all-start = ((bf16[16,1,2,2048]{3,2,1,0:T(2,128)(2,1)}), bf16[16,1,2,2048]{3,2,1,0:T(2,128)(2,1)S(1)}, u32[]{:S(2)}, u32[]{:S(2)}) async-start(bf16[16,1,2,2048]{3,2,1,0:T(2,128)(2,1)} %copy.81), calls=%async_computation | async-start | bytes 262144 | tf_op jit(solution)/shard_map/while/body/eval_jaxpr/all_to_all | solution.py:115
  463.9 9.7 collective-permute-start.4
  467.8 7.8 collective-permute-start.6
  470.0 10.5 %collective-permute-start.8 = (bf16[1,1,2,2048]{3,2,1,0:T(2,128)(2,1)S(1)}, bf16[1,1,2,2048]{3,2,1,0:T(2,128)(2,1)S(1)}, u32[]{:S(2)}, u32[]{:S(2)}) collective-permute-start(bf16[1,1,2,2048]{3,2,1,0:T(2,128)(2,1)S(1)} %get-tuple-element.1152), channel_id=1, source_target_pairs={{0,9},{1,8},{2,11},{3,10},{4,13},{5,12},{6,15},{7,14},{8,1},{9,0},... | collective-permute-start | bytes 24584 | tf_op jit(solution)/shard_map/while/body/eval_jaxpr/ppermute | solution.py:140
  490.5 13.2 %all-to-all-start = ((bf16[16,1,2,2048]{3,2,1,0:T(2,128)(2,1)}), bf16[16,1,2,2048]{3,2,1,0:T(2,128)(2,1)S(1)}, u32[]{:S(2)}, u32[]{:S(2)}) async-start(bf16[16,1,2,2048]{3,2,1,0:T(2,128)(2,1)} %copy.81), calls=%async_computation | async-start | bytes 262144 | tf_op jit(solution)/shard_map/while/body/eval_jaxpr/all_to_all | solution.py:115
  520.6 12.6 %all-to-all-start.1 = ((bf16[16,1,2,2048]{3,2,1,0:T(2,128)(2,1)}), bf16[16,1,2,2048]{3,2,1,0:T(2,128)(2,1)S(1)}, u32[]{:S(2)}, u32[]{:S(2)}) async-start(bf16[16,1,2,2048]{3,2,1,0:T(2,128)(2,1)} %bitcast.444), calls=%async_computation.1 | async-start | bytes 262144 | tf_op jit(solution)/shard_map/while/body/eval_jaxpr/all_to_all | solution.py:193
  538.3 12.0 %all-to-all-start.2 = ((bf16[16,1,2,2048]{3,2,1,0:T(2,128)(2,1)}), bf16[16,1,2,2048]{3,2,1,0:T(2,128)(2,1)S(1)}, u32[]{:S(2)}, u32[]{:S(2)}) async-start(bf16[16,1,2,2048]{3,2,1,0:T(2,128)(2,1)} %copy.84), calls=%async_computation.2 | async-start | bytes 262144 | tf_op jit(solution)/shard_map/while/body/eval_jaxpr/all_to_all | solution.py:198
  565.5 12.6 %all-to-all-start.1 = ((bf16[16,1,2,2048]{3,2,1,0:T(2,128)(2,1)}), bf16[16,1,2,2048]{3,2,1,0:T(2,128)(2,1)S(1)}, u32[]{:S(2)}, u32[]{:S(2)}) async-start(bf16[16,1,2,2048]{3,2,1,0:T(2,128)(2,1)} %bitcast.444), calls=%async_computation.1 | async-start | bytes 262144 | tf_op jit(solution)/shard_map/while/body/eval_jaxpr/all_to_all | solution.py:193
  583.2 12.0 %all-to-all-start.2 = ((bf16[16,1,2,2048]{3,2,1,0:T(2,128)(2,1)}), bf16[16,1,2,2048]{3,2,1,0:T(2,128)(2,1)S(1)}, u32[]{:S(2)}, u32[]{:S(2)}) async-start(bf16[16,1,2,2048]{3,2,1,0:T(2,128)(2,1)} %copy.84), calls=%async_computation.2 | async-start | bytes 262144 | tf_op jit(solution)/shard_map/while/body/eval_jaxpr/all_to_all | solution.py:198
  610.4 12.6 %all-to-all-start.1 = ((bf16[16,1,2,2048]{3,2,1,0:T(2,128)(2,1)}), bf16[16,1,2,2048]{3,2,1,0:T(2,128)(2,1)S(1)}, u32[]{:S(2)}, u32[]{:S(2)}) async-start(bf16[16,1,2,2048]{3,2,1,0:T(2,128)(2,1)} %bitcast.444), calls=%async_computation.1 | async-start | bytes 262144 | tf_op jit(solution)/shard_map/while/body/eval_jaxpr/all_to_all | solution.py:193
  628.1 12.0 %all-to-all-start.2 = ((bf16[16,1,2,2048]{3,2,1,0:T(2,128)(2,1)}), bf16[16,1,2,2048]{3,2,1,0:T(2,128)(2,1)S(1)}, u32[]{:S(2)}, u32[]{:S(2)}) async-start(bf16[16,1,2,2048]{3,2,1,0:T(2,128)(2,1)} %copy.84), calls=%async_computation.2 | async-start | bytes 262144 | tf_op jit(solution)/shard_map/while/body/eval_jaxpr/all_to_all | solution.py:198
  655.3 12.6 %all-to-all-start.1 = ((bf16[16,1,2,2048]{3,2,1,0:T(2,128)(2,1)}), bf16[16,1,2,2048]{3,2,1,0:T(2,128)(2,1)S(1)}, u32[]{:S(2)}, u32[]{:S(2)}) async-start(bf16[16,1,2,2048]{3,2,1,0:T(2,128)(2,1)} %bitcast.444), calls=%async_computation.1 | async-start | bytes 262144 | tf_op jit(solution)/shard_map/while/body/eval_jaxpr/all_to_all | solution.py:193
  673.0 12.0 %all-to-all-start.2 = ((bf16[16,1,2,2048]{3,2,1,0:T(2,128)(2,1)}), bf16[16,1,2,2048]{3,2,1,0:T(2,128)(2,1)S(1)}, u32[]{:S(2)}, u32[]{:S(2)}) async-start(bf16[16,1,2,2048]{3,2,1,0:T(2,128)(2,1)} %copy.84), calls=%async_computation.2 | async-start | bytes 262144 | tf_op jit(solution)/shard_map/while/body/eval_jaxpr/all_to_all | solution.py:198
  700.1 12.6 %all-to-all-start.1 = ((bf16[16,1,2,2048]{3,2,1,0:T(2,128)(2,1)}), bf16[16,1,2,2048]{3,2,1,0:T(2,128)(2,1)S(1)}, u32[]{:S(2)}, u32[]{:S(2)}) async-start(bf16[16,1,2,2048]{3,2,1,0:T(2,128)(2,1)} %bitcast.444), calls=%async_computation.1 | async-start | bytes 262144 | tf_op jit(solution)/shard_map/while/body/eval_jaxpr/all_to_all | solution.py:193
  717.8 12.0 %all-to-all-start.2 = ((bf16[16,1,2,2048]{3,2,1,0:T(2,128)(2,1)}), bf16[16,1,2,2048]{3,2,1,0:T(2,128)(2,1)S(1)}, u32[]{:S(2)}, u32[]{:S(2)}) async-start(bf16[16,1,2,2048]{3,2,1,0:T(2,128)(2,1)} %copy.84), calls=%async_computation.2 | async-start | bytes 262144 | tf_op jit(solution)/shard_map/while/body/eval_jaxpr/all_to_all | solution.py:198
  745.0 12.6 %all-to-all-start.1 = ((bf16[16,1,2,2048]{3,2,1,0:T(2,128)(2,1)}), bf16[16,1,2,2048]{3,2,1,0:T(2,128)(2,1)S(1)}, u32[]{:S(2)}, u32[]{:S(2)}) async-start(bf16[16,1,2,2048]{3,2,1,0:T(2,128)(2,1)} %bitcast.444), calls=%async_computation.1 | async-start | bytes 262144 | tf_op jit(solution)/shard_map/while/body/eval_jaxpr/all_to_all | solution.py:193
  762.7 12.0 %all-to-all-start.2 = ((bf16[16,1,2,2048]{3,2,1,0:T(2,128)(2,1)}), bf16[16,1,2,2048]{3,2,1,0:T(2,128)(2,1)S(1)}, u32[]{:S(2)}, u32[]{:S(2)}) async-start(bf16[16,1,2,2048]{3,2,1,0:T(2,128)(2,1)} %copy.84), calls=%async_computation.2 | async-start | bytes 262144 | tf_op jit(solution)/shard_map/while/body/eval_jaxpr/all_to_all | solution.py:198
  789.9 12.6 %all-to-all-start.1 = ((bf16[16,1,2,2048]{3,2,1,0:T(2,128)(2,1)}), bf16[16,1,2,2048]{3,2,1,0:T(2,128)(2,1)S(1)}, u32[]{:S(2)}, u32[]{:S(2)}) async-start(bf16[16,1,2,2048]{3,2,1,0:T(2,128)(2,1)} %bitcast.444), calls=%async_computation.1 | async-start | bytes 262144 | tf_op jit(solution)/shard_map/while/body/eval_jaxpr/all_to_all | solution.py:193
  807.6 12.0 %all-to-all-start.2 = ((bf16[16,1,2,2048]{3,2,1,0:T(2,128)(2,1)}), bf16[16,1,2,2048]{3,2,1,0:T(2,128)(2,1)S(1)}, u32[]{:S(2)}, u32[]{:S(2)}) async-start(bf16[16,1,2,2048]{3,2,1,0:T(2,128)(2,1)} %copy.84), calls=%async_computation.2 | async-start | bytes 262144 | tf_op jit(solution)/shard_map/while/body/eval_jaxpr/all_to_all | solution.py:198
  834.8 12.6 %all-to-all-start.1 = ((bf16[16,1,2,2048]{3,2,1,0:T(2,128)(2,1)}), bf16[16,1,2,2048]{3,2,1,0:T(2,128)(2,1)S(1)}, u32[]{:S(2)}, u32[]{:S(2)}) async-start(bf16[16,1,2,2048]{3,2,1,0:T(2,128)(2,1)} %bitcast.444), calls=%async_computation.1 | async-start | bytes 262144 | tf_op jit(solution)/shard_map/while/body/eval_jaxpr/all_to_all | solution.py:193
  852.5 12.0 %all-to-all-start.2 = ((bf16[16,1,2,2048]{3,2,1,0:T(2,128)(2,1)}), bf16[16,1,2,2048]{3,2,1,0:T(2,128)(2,1)S(1)}, u32[]{:S(2)}, u32[]{:S(2)}) async-start(bf16[16,1,2,2048]{3,2,1,0:T(2,128)(2,1)} %copy.84), calls=%async_computation.2 | async-start | bytes 262144 | tf_op jit(solution)/shard_map/while/body/eval_jaxpr/all_to_all | solution.py:198
  879.7 12.6 %all-to-all-start.1 = ((bf16[16,1,2,2048]{3,2,1,0:T(2,128)(2,1)}), bf16[16,1,2,2048]{3,2,1,0:T(2,128)(2,1)S(1)}, u32[]{:S(2)}, u32[]{:S(2)}) async-start(bf16[16,1,2,2048]{3,2,1,0:T(2,128)(2,1)} %bitcast.444), calls=%async_computation.1 | async-start | bytes 262144 | tf_op jit(solution)/shard_map/while/body/eval_jaxpr/all_to_all | solution.py:193
  897.3 12.0 %all-to-all-start.2 = ((bf16[16,1,2,2048]{3,2,1,0:T(2,128)(2,1)}), bf16[16,1,2,2048]{3,2,1,0:T(2,128)(2,1)S(1)}, u32[]{:S(2)}, u32[]{:S(2)}) async-start(bf16[16,1,2,2048]{3,2,1,0:T(2,128)(2,1)} %copy.84), calls=%async_computation.2 | async-start | bytes 262144 | tf_op jit(solution)/shard_map/while/body/eval_jaxpr/all_to_all | solution.py:198
  919.0 89.0 %reduce-scatter.2.cloned.1.call-start = ((), (), s32[]{:S(2)}) async-start(), calls=%async_computation.4 | async-start | bytes 786432 | tf_op jit(solution)/shard_map/reduce_scatter | solution.py:258
  (150 other events, 1245.2 us)
Sparse Core Ops, SparseCore 0:
  919.1 87.3 all-reduce.1
Sparse Core Ops, SparseCore 1:
  922.3 13.1 reduce-scatter.1
